TPU v7x, 128 devices: a whole 4x4x4 slice. The times are simulated.
128 devices in a mesh: depth: 16 (over y, x), screen: 8 (over z, core).
Axes of the slice: x: 4, y: 4, z: 4, core: 2. Of those that a mesh axis runs over, the one named last changes fastest.
Arguments:
- block_tile: int32 [16, 16384], P('depth', 'screen'), may hold values from 0 to 511
- block_count: int32 [16, 8], P('depth', 'screen'), may hold values from 256 to 2048, as said below
- slab_rank: int32 [16], replicated, may hold values from 0 to 15, each once
- corner: int32 [2, 16, 16384, 128], P(None, 'depth', 'screen'), may hold values from 0 to 16
- offset: float32 [2, 16, 16384, 128], P(None, 'depth', 'screen'), may hold values from 0.25 to 0.75
- radius: float32 [16, 16384, 128], P('depth', 'screen'), may hold values from 3 to 8
- emission: float32 [3, 16, 16384, 128], P(None, 'depth', 'screen'), may hold values from 0.002 to 0.02
- extinction: float32 [16, 16384, 128], P('depth', 'screen'), may hold values from 0.001 to 0.01
Outputs:
- image_tiles: float32 [512, 32, 128], P(('depth', 'screen'))
Inputs may be any that keep to these rules, and one draw needn't show every extreme that they name: The live slots of a device are its first block_count slots; one device of every draw has all 2048 slots live. `block_tile`: a block holds particles of one tile. `corner`: a footprint box lies inside its tile. `slab_rank`: each slab once.
All inputs are finite; a program needn't handle non-finite values.
Results may differ from a plain program's by a relative error of at most 0.0003.
Values sent between devices are 32-bit elements; how exact they have to be, the bound alone decides.
A program may use at most 128 MiB of HBM per device.

v0:
```python
import functools

import jax
import jax.numpy as jnp
from jax import lax
from jax.experimental import pallas as pl
from jax.experimental.pallas import tpu as pltpu
from jax.sharding import Mesh
from jax.sharding import PartitionSpec as P

SCREEN = ("screen_0", "screen_1")
DEPTH_SCREEN = ("depth", "screen_0", "screen_1")
BLK = 256
UNR = 128

KEPT = 1536
MESH_ID = pl.DeviceIdType.MESH


def share_kernel(tile_ref, count_ref, corner_ref, offset_ref, radius_ref, emission_ref, extinction_ref,
                 tile_out, count_out, corner_out, offset_out, radius_out, emission_out, extinction_out,
                 send_sem, recv_sem):
    mate = 1 - lax.axis_index("screen_1")
    barrier = pltpu.get_barrier_semaphore()
    pl.semaphore_signal(barrier, inc=1, device_id={"screen_1": mate}, device_id_type=MESH_ID)
    pl.semaphore_wait(barrier, 1)
    given = pl.ds(KEPT, tile_ref.shape[1] - KEPT)
    pairs = [
        (tile_ref.at[:, given], tile_out),
        (count_ref, count_out),
        (corner_ref.at[0, :, given], corner_out.at[0]),
        (corner_ref.at[1, :, given], corner_out.at[1]),
        (offset_ref.at[0, :, given], offset_out.at[0]),
        (offset_ref.at[1, :, given], offset_out.at[1]),
        (radius_ref.at[:, given], radius_out),
        (emission_ref.at[0, :, given], emission_out.at[0]),
        (emission_ref.at[1, :, given], emission_out.at[1]),
        (emission_ref.at[2, :, given], emission_out.at[2]),
        (extinction_ref.at[:, given], extinction_out),
    ]
    copies = [
        pltpu.make_async_remote_copy(
            source, goal, send_sem.at[n], recv_sem.at[n], device_id={"screen_1": mate}, device_id_type=MESH_ID)
        for n, (source, goal) in enumerate(pairs)
    ]
    for copy in copies:
        copy.start()
    for copy in copies:
        copy.wait()


def share(block_tile, block_count, corner, offset, radius, emission, extinction):
    num = block_tile.shape[1] - KEPT
    any_spec = pl.BlockSpec(memory_space=pl.ANY)
    def cut(n, dtype):
        return jax.ShapeDtypeStruct((n, 1, num, 128), dtype)
    flat = jax.ShapeDtypeStruct((1, num, 128), jnp.float32)
    return pl.pallas_call(
        share_kernel,
        out_shape=[
            jax.ShapeDtypeStruct((1, num), jnp.int32),
            jax.ShapeDtypeStruct(block_count.shape, jnp.int32),
            cut(2, jnp.int32), cut(2, jnp.float32), flat, cut(3, jnp.float32), flat,
        ],
        in_specs=[any_spec] * 7,
        out_specs=[any_spec] * 7,
        scratch_shapes=[pltpu.SemaphoreType.DMA((11,)), pltpu.SemaphoreType.DMA((11,))],
        compiler_params=pltpu.CompilerParams(collective_id=1, has_side_effects=True),
        name="share",
    )(block_tile, block_count, corner, offset, radius, emission, extinction)


def deposit_kernel(own_steps, tile_ref, count_ref, mate_tile_ref, mate_count_ref, *refs):
    own_refs, mate_refs, (out_ref, pre_ref) = refs[:5], refs[5:10], refs[10:]
    step = pl.program_id(0)
    own = step < own_steps
    first = jnp.minimum(step, own_steps - 1) * BLK
    mate_first = jnp.maximum(step - own_steps, 0) * BLK
    own_live = jnp.minimum(count_ref[0, 0], own_steps * BLK) - first
    mate_live = mate_count_ref[0, 0] - own_steps * BLK - mate_first
    live_num = jnp.where(own, own_live, mate_live)

    @pl.when(step == 0)
    def _():
        def zero(t, c):
            out_ref[t] = jnp.zeros(out_ref.shape[1:], jnp.float32)
            return c
        lax.fori_loop(0, out_ref.shape[0], zero, 0, unroll=8)

    def prepare(corner_ref, offset_ref, radius_ref, emission_ref, extinction_ref):
        live = lax.broadcasted_iota(jnp.int32, (BLK, 128), 0) < live_num
        radius = radius_ref[0]
        h2 = radius * radius
        h4 = h2 * h2
        scale = jnp.where(live, 1.0 / (h4 * h4), 0.0)
        for k in range(2):
            edge = corner_ref[k, 0].astype(jnp.float32)
            pre_ref[2 * k] = edge
            pre_ref[2 * k + 1] = edge + 16.0 * offset_ref[k, 0] - 0.5
        pre_ref[4] = h2
        for c in range(3):
            pre_ref[5 + c] = emission_ref[c, 0] * scale
        pre_ref[8] = extinction_ref[0] * scale

    @pl.when(jnp.logical_and(own, live_num > 0))
    def _():
        prepare(*own_refs)

    @pl.when(jnp.logical_and(jnp.logical_not(own), live_num > 0))
    def _():
        prepare(*mate_refs)

    @pl.when(live_num > 0)
    def _():
        rows = lax.broadcasted_iota(jnp.int32, (16, 128), 0).astype(jnp.float32)
        rows16 = rows.astype(jnp.bfloat16)
        zero16 = jnp.zeros((16, 128), jnp.bfloat16)

        def split(w):
            high = w.astype(jnp.bfloat16)
            low = (w - high.astype(jnp.float32)).astype(jnp.bfloat16)
            return high, low

        def one_group(g, c):
            outs = []
            for u in range(UNR):
                j = g * UNR + u
                def row(a):
                    return jnp.broadcast_to(pre_ref[a, pl.ds(j, 1), :], (16, 128))
                h2r = row(4)
                def bump(k):
                    edge = row(2 * k)
                    mask16 = rows16 < edge.astype(jnp.bfloat16)
                    at = jnp.where(rows < edge, rows + 16.0, rows)
                    s = at - row(2 * k + 1)
                    v = jnp.maximum(h2r - s * s, 0.0)
                    return v * v, mask16
                wx, mx = bump(0)
                wy, my = bump(1)
                def spread(w16, m):
                    return [jnp.where(m, zero16, w16), jnp.where(m, w16, zero16)]
                yh, yl = split(wy)
                lhs = jnp.concatenate(spread(yh, my) + spread(yl, my), 0)
                lhs = jnp.concatenate([lhs, lhs], 1)
                hi, lo = [], []
                for ch in range(4):
                    a, b = split(row(5 + ch) * wx)
                    hi += spread(a, mx)
                    lo += spread(b, mx)
                rhs = jnp.concatenate([jnp.concatenate(hi, 0), jnp.concatenate(lo, 0)], 1)
                outs.append(lax.dot_general(lhs, rhs, (((1,), (1,)), ((), ())), preferred_element_type=jnp.float32))
            for u in range(UNR):
                t = jnp.where(own, tile_ref[0, first + g * UNR + u], mate_tile_ref[0, mate_first + g * UNR + u])
                out_ref[t] += outs[u][:32] + outs[u][32:]
            return c

        groups = lax.div(jnp.minimum(live_num, BLK) + (UNR - 1), UNR)
        lax.fori_loop(0, groups, one_group, 0)


def deposit_all(block_tile, block_count, corner, offset, radius, emission, extinction, tiles=512):
    mate_tile, mate_count, *mate_rest = share(block_tile, block_count, corner, offset, radius, emission, extinction)
    own_steps = KEPT // BLK
    steps = block_tile.shape[1] // BLK
    def own_at(i, tile, count, *unused):
        return jnp.minimum(jnp.minimum(i, own_steps - 1), lax.div(count[0, 0] - 1, BLK))
    def mate_at(i, *unused):
        return jnp.maximum(i - own_steps, 0)
    def specs(at):
        def m4(n):
            return pl.BlockSpec((n, 1, BLK, 128), lambda i, *scalars: (0, 0, at(i, *scalars), 0))
        def m3():
            return pl.BlockSpec((1, BLK, 128), lambda i, *scalars: (0, at(i, *scalars), 0))
        return [m4(2), m4(2), m3(), m4(3), m3()]
    return pl.pallas_call(
        functools.partial(deposit_kernel, own_steps),
        out_shape=pltpu.VMEM((tiles, 32, 128), jnp.float32),
        grid_spec=pltpu.PrefetchScalarGridSpec(
            num_scalar_prefetch=4, grid=(steps,),
            in_specs=specs(own_at) + specs(mate_at),
            out_specs=pl.BlockSpec((tiles, 32, 128), lambda i, *scalars: (0, 0, 0)),
            scratch_shapes=[pltpu.VMEM((9, BLK, 128), jnp.float32)],
        ),
        compiler_params=pltpu.CompilerParams(dimension_semantics=("arbitrary",), vmem_limit_bytes=56000 * 1024),
        name="deposit",
    )(block_tile, block_count, mate_tile, mate_count, corner, offset, radius, emission, extinction, *mate_rest)


def exchange_kernel(rank_ref, partial_ref, image_ref, order_ref, mine, pair, from_up, from_down, via_up, via_down, stack,
                    pair_send, pair_recv, far_send, far_recv, near_send, near_recv, sum_send, sum_recv,
                    stack_send, stack_recv):
    d = lax.axis_index("depth")
    z = lax.axis_index("screen_0")
    core = lax.axis_index("screen_1")
    mate = 1 - core
    y, x = lax.div(d, 4), lax.rem(d, 4)
    z_up, z_down, z_far = lax.rem(z + 1, 4), lax.rem(z + 3, 4), lax.rem(z + 2, 4)
    turns = (2, 1, 3, 0)
    steps = (2, 3, 1, 0)
    summed_up = (2, 1)
    others = [(ry, rx) for ry in turns for rx in (2, 1, 3, 0) if (ry, rx) != (0, 0)]

    def away(ry, rx):
        return lax.rem(y + ry, 4) * 4 + lax.rem(x + rx, 4)

    def row(ry):
        return lax.rem(y + ry, 4) * 4

    barrier = pltpu.get_barrier_semaphore()
    pl.semaphore_signal(barrier, inc=1, device_id={"screen_1": mate}, device_id_type=MESH_ID)
    pl.semaphore_signal(barrier, inc=1, device_id={"screen_0": z_up}, device_id_type=MESH_ID)
    pl.semaphore_signal(barrier, inc=1, device_id={"screen_0": z_down}, device_id_type=MESH_ID)
    for ry, rx in others:
        pl.semaphore_signal(barrier, inc=1, device_id={"depth": away(ry, rx)}, device_id_type=MESH_ID)

    places = (z_far, z_up, z_down, z)

    def pair_copy(p, g):
        rows = pl.ds(row(g), 4)
        return pltpu.make_async_remote_copy(
            partial_ref.at[rows, places[p], mate], pair.at[rows, places[p]],
            pair_send.at[p, g], pair_recv.at[p, g], device_id={"screen_1": mate}, device_id_type=MESH_ID)

    def line_copy(ry, rx, place, goal, to_up, send, recv):
        to, n = away(ry, rx), (2, 1, 3, 0).index(rx) % 2
        return pltpu.make_async_remote_copy(
            mine.at[to, place], goal.at[to], send.at[to_up, ry, n], recv.at[to_up, ry, n],
            device_id={"screen_0": z_up if to_up else z_down}, device_id_type=MESH_ID)

    def far_copy(ry, rx):
        to_up = int(rx in summed_up)
        return line_copy(ry, rx, z_far, via_up if to_up else via_down, to_up, far_send, far_recv)

    def near_copy(ry, rx):
        to_up = int(rx not in summed_up)
        return line_copy(ry, rx, z_up if to_up else z_down, from_up if to_up else from_down, to_up,
                         near_send, near_recv)

    def sum_copy(ry, rx):
        to_up = int(rx in summed_up)
        return line_copy(ry, rx, z_up if to_up else z_down, from_up if to_up else from_down, to_up,
                         sum_send, sum_recv)

    def stack_copy(ry, rx):
        to = away(ry, rx)
        return pltpu.make_async_remote_copy(
            mine.at[to, z], stack.at[d], stack_send.at[ry, rx], stack_recv.at[ry, rx],
            device_id={"depth": to}, device_id_type=MESH_ID)

    def add_in(first, num, place, terms):
        def one(i, c):
            total = terms[0](first + i)
            for term in terms[1:]:
                total = total + term(first + i)
            mine[first + i, place] = total
            return c
        lax.fori_loop(0, num, one, 0)

    pl.semaphore_wait(barrier, 18)
    for p in range(4):
        for g in turns:
            pair_copy(p, g).start()

    for p in range(16):
        slab = 0
        for j in range(1, 16):
            slab = jnp.where(rank_ref[j] == p, j, slab)
        order_ref[p] = slab

    def take_pair(p, g):
        pair_copy(p, g).wait_recv()

    for g in turns:
        take_pair(0, g)
        add_in(row(g), 4, z_far, [lambda i: partial_ref[i, z_far, core], lambda i: pair[i, z_far]])
        for rx in steps:
            far_copy(g, rx).start()
    for g in turns:
        for p, to_up in ((1, 1), (2, 0)):
            take_pair(p, g)
            add_in(row(g), 4, places[p], [
                lambda i, p=p: partial_ref[i, places[p], core], lambda i, p=p: pair[i, places[p]]])
            for rx in steps:
                if int(rx not in summed_up) == to_up:
                    near_copy(g, rx).start()
    for g in turns:
        for rx in steps:
            far_copy(g, rx).wait_recv()
            to_up = int(rx in summed_up)
            via, place = (via_up, z_up) if to_up else (via_down, z_down)
            add_in(away(g, rx), 1, place, [
                lambda i, place=place: mine[i, place], lambda i, via=via: via[i]])
            sum_copy(g, rx).start()
    for g in turns:
        take_pair(3, g)
        for rx in steps:
            near_copy(g, rx).wait_recv()
            sum_copy(g, rx).wait_recv()
            add_in(away(g, rx), 1, z, [
                lambda i: partial_ref[i, z, core], lambda i: pair[i, z], lambda i: from_up[i], lambda i: from_down[i]])
            if (g, rx) != (0, 0):
                stack_copy(g, rx).start()
    stack[d] = mine[d, z]
    for ry, rx in others:
        stack_copy(ry, rx).wait_recv()

    lane = lax.broadcasted_iota(jnp.int32, (2, 32, 128), 2)

    for t in (0, 2):
        def one_slab(p, carry, t=t):
            prior, light = carry
            value = stack[order_ref[p], pl.ds(t, 2)]
            own = jnp.where(lane >= 96, value, 0.0)
            twice = own + pltpu.roll(own, 32, 2)
            optical = twice + pltpu.roll(twice, 64, 2)
            light = light + jnp.exp(-(prior + 0.5 * optical)) * value
            return prior + optical, light
        zero = jnp.zeros((2, 32, 128), jnp.float32)
        prior, light = lax.fori_loop(0, 16, one_slab, (zero, zero), unroll=4)
        image_ref[pl.ds(t, 2)] = jnp.where(lane >= 96, 1.0 - jnp.exp(-prior), light)

    for g in turns:
        for p in range(4):
            pair_copy(p, g).wait_send()
        for rx in steps:
            far_copy(g, rx).wait_send()
            near_copy(g, rx).wait_send()
            sum_copy(g, rx).wait_send()
    for ry, rx in others:
        stack_copy(ry, rx).wait_send()


def exchange(partial_value, slab_rank):
    dma = pltpu.SemaphoreType.DMA
    return pl.pallas_call(
        exchange_kernel,
        out_shape=jax.ShapeDtypeStruct((4, 32, 128), jnp.float32),
        in_specs=[pl.BlockSpec(memory_space=pltpu.SMEM), pl.BlockSpec(memory_space=pltpu.VMEM)],
        out_specs=pl.BlockSpec(memory_space=pltpu.VMEM),
        scratch_shapes=[
            pltpu.SMEM((16,), jnp.int32),
            pltpu.VMEM((16, 4, 4, 32, 128), jnp.float32),
            pltpu.VMEM((16, 4, 4, 32, 128), jnp.float32),
            pltpu.VMEM((16, 4, 32, 128), jnp.float32),
            pltpu.VMEM((16, 4, 32, 128), jnp.float32),
            pltpu.VMEM((16, 4, 32, 128), jnp.float32),
            pltpu.VMEM((16, 4, 32, 128), jnp.float32),
            pltpu.VMEM((16, 4, 32, 128), jnp.float32),
            dma((4, 4)), dma((4, 4)),
            *[dma((2, 4, 2))] * 6,
            dma((4, 4)), dma((4, 4)),
        ],
        compiler_params=pltpu.CompilerParams(collective_id=0, has_side_effects=True, vmem_limit_bytes=24 * 2**20),
        name="exchange",
    )(slab_rank, partial_value.reshape(16, 4, 2, 4, 32, 128))


def shards(block_tile, block_count, slab_rank, corner, offset, radius, emission, extinction):
    partial_value = deposit_all(
        block_tile, block_count, corner, offset, radius, emission, extinction
    )
    return exchange(partial_value, slab_rank)


def solution(mesh):
    torus = Mesh(mesh.devices.reshape(mesh.shape["depth"], 4, 2), ("depth", "screen_0", "screen_1"))
    placed = (
        P("depth", SCREEN),
        P("depth", SCREEN),
        P(),
        P(None, "depth", SCREEN, None),
        P(None, "depth", SCREEN, None),
        P("depth", SCREEN, None),
        P(None, "depth", SCREEN, None),
        P("depth", SCREEN, None),
    )
    return jax.shard_map(
        shards, mesh=torus, in_specs=placed, out_specs=P(DEPTH_SCREEN, None, None), check_vma=False
    )
```

profile of v0, /device:TPU:33, one launch (start us, length us, event | category | flops | bytes accessed | tf_op | source)
XLA Modules:
  0.0 98.8 jit_solution(12366603946723032284)
XLA Ops:
  0.7 5.5 %share.1 = (s32[1,512]{1,0:T(1,128)}, s32[1,1]{1,0:T(1,128)}, s32[2,1,512,128]{3,2,1,0:T(8,128)}, f32[2,1,512,128]{3,2,1,0:T(8,128)}, f32[1,512,128]{2,1,0:T(8,1...) custom-call(s32[1,2048]{1,0:T(1,128)} %tile_ref.3, s32[1,1]{1,0:T(1,128)S(6)} %copy.10.count_ref, ...), custom_call_target="tpu_custom_call" | custom-call | tf_op jit(solution)/shard_map/share/pallas_call | solution.py:58
  6.1 0.0 copy-start
  6.1 18.5 %deposit.1 = f32[512,32,128]{2,1,0:T(8,128)S(1)} custom-call(s32[1,2048]{1,0:T(1,128)} %tile_ref.3, s32[1,1]{1,0:T(1,128)S(6)} %copy.10.count_ref, s32[1,512]{1,0:T(1,128)} %get-tuple-element.12.mate_tile_ref, s32[1,1]{1,0:T(1,128)} %get-tuple-element.13.mate_count_ref, s32[2,1,2048,128]{3,2,1,0:T(8,128)} %refs_0_.1, f32[2,1,2048,128]{3,2,1,0:T(8,128)} %refs_1_.1, ...), custom_call_target="tpu_custom_call" | custom-call | tf_op jit(solution)/shard_map/deposit/pallas_call | solution.py:175
  24.6 0.0 copy-done
  24.7 73.5 %exchange.1 = f32[4,32,128]{2,1,0:T(8,128)S(1)} custom-call(s32[16]{0:T(128)S(1)} %copy-done, f32[16,4,2,4,32,128]{5,4,3,2,1,0:T(8,128)S(1)} %bitcast.1), custom_call_target="tpu_custom_call" | custom-call | tf_op jit(solution)/shard_map/exchange/pallas_call | solution.py:335
  98.1 0.6 copy.11
Async XLA Ops:
  6.1 18.5 %copy-start = (s32[16]{0:T(128)S(1)}, s32[16]{0:T(128)}, u32[]{:S(2)}) copy-start(s32[16]{0:T(128)} %rank_ref.1) | copy-start | bytes 196
where the time goes:
time: 98.2 us; the launch traced here: 98.8 us
  Pallas kernels  97.5 us (99%)
    pallas_call x1, Pallas kernels, exchange(): pl.pallas_call(exchange_kernel, out_shape=jax.ShapeDtypeStruct((4, 32, 12...  73.5 us
    pallas_call x1, Pallas kernels, deposit_all(): pl.pallas_call(functools.partial(deposit_kernel, own_steps), out_shape=pl...  18.5 us
    pallas_call x1, Pallas kernels, share(): pl.pallas_call(share_kernel, out_shape=[jax.ShapeDtypeStruct((1, num), jn...  5.47 us

commit v1 on v0

--- a/solution.py
+++ b/solution.py
@@ -11,7 +11,7 @@
 SCREEN = ("screen_0", "screen_1")
 DEPTH_SCREEN = ("depth", "screen_0", "screen_1")
 BLK = 256
-UNR = 128
+UNR = 256
 
 KEPT = 1536
 MESH_ID = pl.DeviceIdType.MESH

time: 98.2 us -> 97.9 us (level)
  the two profiles are of different devices: /device:TPU:33 before, /device:TPU:0 now
where the time goes in v1:
time: 97.9 us; the launch traced here: 96.1 us
  Pallas kernels  94.7 us (97%)
    pallas_call x1, Pallas kernels, exchange(): pl.pallas_call(exchange_kernel, out_shape=jax.ShapeDtypeStruct((4, 32, 12...  59.2 us
    pallas_call x1, Pallas kernels, deposit_all(): pl.pallas_call(functools.partial(deposit_kernel, own_steps), out_shape=pl...  30.4 us
    pallas_call x1, Pallas kernels, share(): pl.pallas_call(share_kernel, out_shape=[jax.ShapeDtypeStruct((1, num), jn...  5.17 us

profile of v1, /device:TPU:0, one launch (start us, length us, event | category | flops | bytes accessed | tf_op | source)
XLA Modules:
  0.0 96.1 jit_solution(15683778767077940067)
XLA Ops:
  0.7 5.2 %share.1 = (s32[1,512]{1,0:T(1,128)}, s32[1,1]{1,0:T(1,128)}, s32[2,1,512,128]{3,2,1,0:T(8,128)}, f32[2,1,512,128]{3,2,1,0:T(8,128)}, f32[1,512,128]{2,1,0:T(8,1...) custom-call(s32[1,2048]{1,0:T(1,128)} %tile_ref.3, s32[1,1]{1,0:T(1,128)S(6)} %copy.10.count_ref, ...), custom_call_target="tpu_custom_call" | custom-call | tf_op jit(solution)/shard_map/share/pallas_call | solution.py:58
  5.8 0.0 copy-start
  5.8 30.4 %deposit.1 = f32[512,32,128]{2,1,0:T(8,128)S(1)} custom-call(s32[1,2048]{1,0:T(1,128)} %tile_ref.3, s32[1,1]{1,0:T(1,128)S(6)} %copy.10.count_ref, s32[1,512]{1,0:T(1,128)} %get-tuple-element.12.mate_tile_ref, s32[1,1]{1,0:T(1,128)} %get-tuple-element.13.mate_count_ref, s32[2,1,2048,128]{3,2,1,0:T(8,128)} %refs_0_.1, f32[2,1,2048,128]{3,2,1,0:T(8,128)} %refs_1_.1, ...), custom_call_target="tpu_custom_call" | custom-call | tf_op jit(solution)/shard_map/deposit/pallas_call | solution.py:175
  36.3 0.0 copy-done
  36.3 59.2 %exchange.1 = f32[4,32,128]{2,1,0:T(8,128)S(1)} custom-call(s32[16]{0:T(128)S(1)} %copy-done, f32[16,4,2,4,32,128]{5,4,3,2,1,0:T(8,128)S(1)} %bitcast.1), custom_call_target="tpu_custom_call" | custom-call | tf_op jit(solution)/shard_map/exchange/pallas_call | solution.py:335
  95.4 0.6 copy.11
Async XLA Ops:
  5.8 30.4 %copy-start = (s32[16]{0:T(128)S(1)}, s32[16]{0:T(128)}, u32[]{:S(2)}) copy-start(s32[16]{0:T(128)} %rank_ref.1) | copy-start | bytes 196
